TPU v7x, 256 devices: a whole 4x4x8 slice. The times are simulated.
256 devices in a mesh: ep: 32 (over z, y), dp: 8 (over x, core).
Axes of the slice: x: 4, y: 4, z: 8, core: 2. Of those that a mesh axis runs over, the one named last changes fastest.
Arguments:
- tokens: bfloat16 [8192, 512], P(('dp', 'ep'))
- d_out: bfloat16 [8192, 512], P(('dp', 'ep'))
- expert_ids: int32 [2, 8192, 6], P(None, ('dp', 'ep'))
- gate_vals: float32 [2, 8192, 6], P(None, ('dp', 'ep'))
- w_mix: bfloat16 [2, 512, 512], replicated
- w_gate: bfloat16 [2, 64, 512, 352], P(None, 'ep')
- w_up: bfloat16 [2, 64, 512, 352], P(None, 'ep')
- w_down: bfloat16 [2, 64, 352, 512], P(None, 'ep')
Outputs:
- output 1: bfloat16 [8192, 512], P(('dp', 'ep'))
- output 2: bfloat16 [8192, 512], P(('dp', 'ep'))
- output 3: bfloat16 [2, 512, 512], replicated
- output 4: bfloat16 [2, 64, 512, 352], P(None, 'ep')
- output 5: bfloat16 [2, 64, 512, 352], P(None, 'ep')
- output 6: bfloat16 [2, 64, 352, 512], P(None, 'ep')
All inputs are finite; a program needn't handle non-finite values.
Results may differ from a plain program's by a relative error of at most 0.02.
Values are sent between devices in bfloat16 or wider.
A program may use at most 768 MiB of HBM per device.

v0:
```python
import jax
import jax.numpy as jnp
from jax import lax
from jax.sharding import PartitionSpec as P

CAP_FACTOR = 3


def silu_parts(pre_gate):
    sig_val = jax.nn.sigmoid(pre_gate)
    return pre_gate * sig_val, sig_val * (1.0 + pre_gate * (1.0 - sig_val))


def route_tables(expert_ids, n_experts, capacity):
    flat_ids = expert_ids.reshape(-1)
    n_copies = flat_ids.shape[0]
    sort_order = jnp.argsort(flat_ids, stable=True)
    counts = jnp.bincount(flat_ids, length=n_experts)
    starts = jnp.cumsum(counts) - counts
    slot_pos = jnp.arange(capacity)
    src_copy = sort_order[jnp.minimum(starts[:, None] + slot_pos[None, :], n_copies - 1)]
    is_valid = slot_pos[None, :] < counts[:, None]
    sorted_ids = flat_ids[sort_order]
    rows_sorted = sorted_ids * capacity + jnp.arange(n_copies) - starts[sorted_ids]
    copy_row = jnp.zeros_like(flat_ids).at[sort_order].set(rows_sorted)
    return src_copy, is_valid, copy_row


def layer_forward(x_in, expert_ids, gate_vals, w_mix, w_gate, w_up, w_down, n_experts, capacity):
    tok_local, d_model = x_in.shape
    top_k = expert_ids.shape[1]
    n_local = w_gate.shape[0]
    mixed = x_in.astype(jnp.float32) + jnp.dot(x_in, w_mix, preferred_element_type=jnp.float32)
    u_act = mixed.astype(jnp.bfloat16)
    src_copy, is_valid, copy_row = route_tables(expert_ids, n_experts, capacity)
    send_buf = jnp.where(is_valid[:, :, None], u_act[src_copy // top_k], 0)
    send_buf = send_buf.reshape(n_experts // n_local, n_local, capacity, d_model)
    recv_buf = lax.all_to_all(send_buf, 'ep', 0, 0, tiled=True)
    pre_gate = jnp.einsum('secd,edf->secf', recv_buf, w_gate, preferred_element_type=jnp.float32)
    pre_up = jnp.einsum('secd,edf->secf', recv_buf, w_up, preferred_element_type=jnp.float32)
    act, _ = silu_parts(pre_gate)
    hidden = (act * pre_up).astype(jnp.bfloat16)
    out_buf = jnp.einsum('secf,efd->secd', hidden, w_down, preferred_element_type=jnp.float32).astype(jnp.bfloat16)
    back_buf = lax.all_to_all(out_buf, 'ep', 0, 0, tiled=True).reshape(n_experts * capacity, d_model)
    out_copy = back_buf[copy_row].reshape(tok_local, top_k, d_model)
    y_out = u_act.astype(jnp.float32) + jnp.sum(gate_vals[:, :, None] * out_copy.astype(jnp.float32), axis=1)
    saved = (x_in, src_copy, is_valid, copy_row, recv_buf, pre_gate, pre_up, hidden)
    return y_out.astype(jnp.bfloat16), saved


def layer_backward(saved, d_y, gate_vals, w_mix, w_gate, w_up, w_down):
    x_in, src_copy, is_valid, copy_row, recv_buf, pre_gate, pre_up, hidden = saved
    tok_local, d_model = d_y.shape
    top_k = gate_vals.shape[1]
    n_experts, capacity = is_valid.shape
    g_dy = (gate_vals[:, :, None] * d_y.astype(jnp.float32)[:, None, :]).astype(jnp.bfloat16)
    g_dy = g_dy.reshape(tok_local * top_k, d_model)
    send_grad = jnp.where(is_valid[:, :, None], g_dy[src_copy], 0).reshape(recv_buf.shape)
    recv_grad = lax.all_to_all(send_grad, 'ep', 0, 0, tiled=True)
    d_hidden = jnp.einsum('secd,efd->secf', recv_grad, w_down, preferred_element_type=jnp.float32)
    act, act_slope = silu_parts(pre_gate)
    d_pre_gate = (d_hidden * pre_up * act_slope).astype(jnp.bfloat16)
    d_pre_up = (d_hidden * act).astype(jnp.bfloat16)
    d_recv = (jnp.einsum('secf,edf->secd', d_pre_gate, w_gate, preferred_element_type=jnp.float32)
              + jnp.einsum('secf,edf->secd', d_pre_up, w_up, preferred_element_type=jnp.float32)).astype(jnp.bfloat16)
    g_gate = jnp.einsum('secd,secf->edf', recv_buf, d_pre_gate, preferred_element_type=jnp.float32).astype(jnp.bfloat16)
    g_up = jnp.einsum('secd,secf->edf', recv_buf, d_pre_up, preferred_element_type=jnp.float32).astype(jnp.bfloat16)
    g_down = jnp.einsum('secf,secd->efd', hidden, recv_grad, preferred_element_type=jnp.float32).astype(jnp.bfloat16)
    g_gate = lax.psum(g_gate, 'dp')
    g_up = lax.psum(g_up, 'dp')
    g_down = lax.psum(g_down, 'dp')
    d_back = lax.all_to_all(d_recv, 'ep', 0, 0, tiled=True).reshape(n_experts * capacity, d_model)
    d_copy = d_back[copy_row].reshape(tok_local, top_k, d_model)
    d_u = (d_y.astype(jnp.float32)
           + jnp.sum(gate_vals[:, :, None] * d_copy.astype(jnp.float32), axis=1)).astype(jnp.bfloat16)
    g_mix = jnp.einsum('td,te->de', x_in, d_u, preferred_element_type=jnp.float32).astype(jnp.bfloat16)
    g_mix = lax.psum(g_mix, ('dp', 'ep'))
    d_x = (d_u.astype(jnp.float32)
           + jnp.einsum('te,de->td', d_u, w_mix, preferred_element_type=jnp.float32)).astype(jnp.bfloat16)
    return d_x, (g_mix, g_gate, g_up, g_down)


def stack_part(grads, index):
    return jnp.stack([entry[index] for entry in grads])


def solution(mesh):
    ep_size = mesh.shape['ep']
    tok_spec = P(('dp', 'ep'), None)
    route_spec = P(None, ('dp', 'ep'), None)
    whole_spec = P(None, None, None)
    expert_spec = P(None, 'ep', None, None)

    def device_step(tokens, d_out, expert_ids, gate_vals, w_mix, w_gate, w_up, w_down):
        n_layers = w_mix.shape[0]
        n_experts = w_gate.shape[1] * ep_size
        tok_local = tokens.shape[0]
        top_k = expert_ids.shape[2]
        capacity = (CAP_FACTOR * tok_local * top_k + n_experts - 1) // n_experts
        layer_in = tokens
        saved_all = []
        for layer in range(n_layers):
            layer_in, saved = layer_forward(layer_in, expert_ids[layer], gate_vals[layer], w_mix[layer],
                                            w_gate[layer], w_up[layer], w_down[layer], n_experts, capacity)
            saved_all.append(saved)
        d_y = d_out
        grads = []
        for layer in reversed(range(n_layers)):
            d_y, grad_set = layer_backward(saved_all[layer], d_y, gate_vals[layer], w_mix[layer],
                                           w_gate[layer], w_up[layer], w_down[layer])
            grads.insert(0, grad_set)
        return (layer_in, d_y, stack_part(grads, 0), stack_part(grads, 1),
                stack_part(grads, 2), stack_part(grads, 3))

    return jax.shard_map(device_step, mesh=mesh,
                         in_specs=(tok_spec, tok_spec, route_spec, route_spec, whole_spec,
                                   expert_spec, expert_spec, expert_spec),
                         out_specs=(tok_spec, tok_spec, whole_spec, expert_spec, expert_spec, expert_spec),
                         check_vma=False)
```

profile of v0, /device:TPU:1, one launch (start us, length us, event | category | flops | bytes accessed | tf_op | source)
XLA Modules:
  0.0 617.2 jit_solution(11911069317639058267)
XLA Ops:
  8.3 1.9 scatter_custom_fusion
  10.9 3.2 sort.31
  14.1 3.9 gather_fusion
  19.1 2.8 gather_fusion.1
  22.5 1.5 copy.120
  24.0 12.2 %all-to-all-start = ((bf16[32,2,9,512]{3,1,2,0:T(2,128)(2,1)}), bf16[32,2,9,512]{3,1,2,0:T(2,128)(2,1)S(1)}, u32[]{:S(2)}, u32[]{:S(2)}) async-start(bf16[32,2,9,512]{3,1,2,0:T(2,128)(2,1)} %copy.120), calls=%async_computation | async-start | bytes 1179648 | tf_op jit(solution)/shard_map/all_to_all | solution.py:38
  36.9 1.9 scatter_custom_fusion.2
  40.0 3.2 sort.32
  43.2 3.9 gather_fusion.5
  48.2 2.7 gather_fusion.10
  50.9 1.2 gather.75
  52.2 1.6 gather_fusion.2
  54.3 1.4 multiply_convert_fusion.5
  57.0 1.4 copy.123
  58.4 9.5 %all-to-all-start.1 = ((bf16[32,2,9,512]{3,1,2,0:T(2,128)(2,1)}), bf16[32,2,9,512]{3,1,2,0:T(2,128)(2,1)S(1)}, u32[]{:S(2)}, u32[]{:S(2)}) async-start(bf16[32,2,9,512]{3,1,2,0:T(2,128)(2,1)} %copy.123), calls=%async_computation.1 | async-start | bytes 1179648 | tf_op jit(solution)/shard_map/all_to_all | solution.py:44
  68.0 1.6 gather_fusion.3
  71.1 13.7 %all-to-all-done.1 = bf16[32,2,9,512]{3,1,2,0:T(2,128)(2,1)S(1)} async-done(((bf16[32,2,9,512]{3,1,2,0:T(2,128)(2,1)}), bf16[32,2,9,512]{3,1,2,0:T(2,128)(2,1)S(1)}, u32[]{:S(2)}, u32[]{:S(2)}) %all-to-all-start.1) | async-done | bytes 589856 | tf_op jit(solution)/shard_map/all_to_all | solution.py:44
  86.0 1.4 reshape.400
  88.7 1.2 fusion.21
  90.0 2.7 gather_fusion.6
  93.9 2.7 broadcast_select_fusion
  96.7 1.5 copy.131
  98.1 6.2 %all-to-all-start.2 = ((bf16[32,2,9,512]{3,1,2,0:T(2,128)(2,1)}), bf16[32,2,9,512]{3,1,2,0:T(2,128)(2,1)S(1)}, u32[]{:S(2)}, u32[]{:S(2)}) async-start(bf16[32,2,9,512]{3,1,2,0:T(2,128)(2,1)} %copy.131), calls=%async_computation.2 | async-start | bytes 1179648 | tf_op jit(solution)/shard_map/all_to_all | solution.py:38
  104.3 2.7 copy.137
  107.1 14.1 %all-to-all-done.2 = bf16[32,2,9,512]{3,1,2,0:T(2,128)(2,1)S(1)} async-done(((bf16[32,2,9,512]{3,1,2,0:T(2,128)(2,1)}), bf16[32,2,9,512]{3,1,2,0:T(2,128)(2,1)S(1)}, u32[]{:S(2)}, u32[]{:S(2)}) %all-to-all-start.2) | async-done | bytes 589856 | tf_op jit(solution)/shard_map/all_to_all | solution.py:38
  121.1 5.6 all-to-all-start.4
  126.7 1.4 convolution_bitcast_fusion.9
  128.1 15.1 %all-to-all-done.4 = bf16[32,2,9,512]{3,1,2,0:T(2,128)(2,1)S(1)} async-done(((bf16[32,2,9,512]{3,1,2,0:T(2,128)(2,1)}), bf16[32,2,9,512]{3,1,2,0:T(2,128)(2,1)S(1)}, u32[]{:S(2)}, u32[]{:S(2)}) %all-to-all-start.4) | async-done | bytes 589856 | tf_op jit(solution)/shard_map/all_to_all | solution.py:59
  143.2 1.8 convolution_bitcast_fusion.7
  145.1 2.6 multiply_convert_fusion.4
  149.0 1.4 copy.139
  150.4 5.5 all-to-all-start.5
  155.9 1.7 fusion.15
  157.7 1.4 copy.134
  159.1 13.7 %all-to-all-done.5 = bf16[32,2,9,512]{3,1,2,0:T(2,128)(2,1)S(1)} async-done(((bf16[32,2,9,512]{3,1,2,0:T(2,128)(2,1)}), bf16[32,2,9,512]{3,1,2,0:T(2,128)(2,1)S(1)}, u32[]{:S(2)}, u32[]{:S(2)}) %all-to-all-start.5) | async-done | bytes 589856 | tf_op jit(solution)/shard_map/all_to_all | solution.py:72
  172.8 4.9 all-to-all-start.3
  178.3 1.6 gather_fusion.7
  180.0 1.6 gather_fusion.8
  181.6 1.4 scatter_custom_fusion.3
  184.3 1.4 reshape.404
  187.7 6.2 %all-to-all-done.3 = bf16[32,2,9,512]{3,1,2,0:T(2,128)(2,1)} async-done(((bf16[32,2,9,512]{3,1,2,0:T(2,128)(2,1)}), bf16[32,2,9,512]{3,1,2,0:T(2,128)(2,1)}, u32[]{:S(2)}, u32[]{:S(2)}) %all-to-all-start.3) | async-done | bytes 589856 | tf_op jit(solution)/shard_map/all_to_all | solution.py:44
  193.9 2.2 copy.135
  196.1 1.4 reshape.403
  198.6 2.1 multiply_reduce_fusion.1
  200.7 1.3 fusion.23
  204.0 2.7 gather_fusion.12
  208.0 1.5 broadcast_select_fusion.2
  210.2 19.7 %all_to_all.40 = bf16[32,2,9,512]{3,1,2,0:T(2,128)(2,1)S(1)} all-to-all(bf16[32,2,9,512]{3,1,2,0:T(2,128)(2,1)S(1)} %copy.142), channel_id=1, replica_groups=mesh['ep'=32,'dp'=8] {'ep'}, dimensions={0} | all-to-all | bytes 1179648 | tf_op jit(solution)/shard_map/all_to_all | solution.py:59
  233.6 1.4 copy.144
  235.0 5.4 all-to-all-start.7
  240.5 1.4 fusion.10
  242.0 2.5 fusion.8
  244.4 1.5 fusion.12
  247.1 8.0 %all-to-all-done.7 = bf16[32,2,9,512]{3,1,2,0:T(2,128)(2,1)S(1)} async-done(((bf16[32,2,9,512]{3,1,2,0:T(2,128)(2,1)}), bf16[32,2,9,512]{3,1,2,0:T(2,128)(2,1)S(1)}, u32[]{:S(2)}, u32[]{:S(2)}) %all-to-all-start.7) | async-done | bytes 589856 | tf_op jit(solution)/shard_map/all_to_all | solution.py:72
  258.4 1.4 fusion.11
  259.8 1.5 fusion.9
  261.3 1.5 fusion.13
  265.1 258.8 %all-reduce.5.cloned.1.call-done = (bf16[1,512,512]{1,2,0:T(8,128)(2,1)}, bf16[1,512,512]{1,2,0:T(8,128)(2,1)}) async-done(((bf16[1,512,512]{1,2,0:T(8,128)(2,1)}, bf16[1,512,512]{1,2,0:T(8,128)(2,1)}), (bf16[1,512,512]{1,2,0:T(8,128)(2,1)}, bf16[1,512,512]{1,2,0:T(8,128)(2,1)})) %all-reduce.5.cloned.1.call-update) | async-done | bytes 1048592 | tf_op jit(solution)/shard_map/psum | solution.py:77
  524.0 1.3 pad_maximum_fusion.3
  525.3 1.3 copy.153
  526.6 77.6 %all-reduce.7.cloned.1.call-done = (bf16[1,2,512,352]{2,3,1,0:T(8,128)(2,1)}, bf16[1,2,512,352]{2,3,1,0:T(8,128)(2,1)}, bf16[1,2,512,352]{2,3,1,0:T(8,128)(2,1)}...) async-done(((bf16[1,2,512,352]{2,3,1,0:T(8,128)(2,1)}, bf16[1,2,512,352]{2,3,1,0:T(8,128)(2,1)}, ...) | async-done | bytes 4325392 | tf_op jit(solution)/shard_map/psum | solution.py:69
  604.2 2.7 pad_maximum_fusion
  606.9 1.2 pad_maximum_fusion.1
  608.7 1.2 pad_maximum_fusion.2
  (202 shorter events, 34.4 us)
Async XLA Ops:
  14.1 4.9 copy-start.1
  14.1 4.9 copy-start.37
  22.3 1.7 copy-start.34
  22.5 13.8 %copy-start.29 = (bf16[32,512]{1,0:T(8,128)(2,1)S(1)}, bf16[32,512]{1,0:T(8,128)(2,1)}, u32[]{:S(2)}) copy-start(bf16[32,512]{1,0:T(8,128)(2,1)} %param.9) | copy-start | bytes 98308
  24.0 12.4 %copy-start.42 = (f32[2,32,6]{1,0,2:T(2,128)S(1)}, f32[2,32,6]{1,0,2:T(2,128)}, u32[]{:S(2)}) copy-start(f32[2,32,6]{1,0,2:T(2,128)} %param.11) | copy-start | bytes 4612
  24.0 29.8 %all-to-all-start = ((bf16[32,2,9,512]{3,1,2,0:T(2,128)(2,1)}), bf16[32,2,9,512]{3,1,2,0:T(2,128)(2,1)S(1)}, u32[]{:S(2)}, u32[]{:S(2)}) async-start(bf16[32,2,9,512]{3,1,2,0:T(2,128)(2,1)} %copy.120), calls=%async_computation | async-start | bytes 1179648 | tf_op jit(solution)/shard_map/all_to_all | solution.py:38
  36.5 3.6 copy-start.36
  50.9 2.9 copy-start
  52.2 2.1 copy-start.12
  54.3 1.4 copy-start.15
  54.3 2.2 copy-start.27
  55.7 0.8 copy-start.44
  57.0 13.9 %copy-start.40 = (s32[64,9,1]{1,0,2:T(8,128)S(1)}, s32[64,9,1]{1,0,2:T(8,128)}, u32[]{:S(2)}) copy-start(s32[64,9,1]{1,0,2:T(8,128)} %get-tuple-element.58) | copy-start | bytes 6916
  58.4 12.6 %copy-start.41 = (s32[32,2]{1,0:T(8,128)S(1)}, s32[32,2]{1,0:T(8,128)}, u32[]{:S(2)}) copy-start(s32[32,2]{1,0:T(8,128)} %lt.151) | copy-start | bytes 772
  58.4 26.4 %all-to-all-start.1 = ((bf16[32,2,9,512]{3,1,2,0:T(2,128)(2,1)}), bf16[32,2,9,512]{3,1,2,0:T(2,128)(2,1)S(1)}, u32[]{:S(2)}, u32[]{:S(2)}) async-start(bf16[32,2,9,512]{3,1,2,0:T(2,128)(2,1)} %copy.123), calls=%async_computation.1 | async-start | bytes 1179648 | tf_op jit(solution)/shard_map/all_to_all | solution.py:44
  70.8 106.8 %copy-start.32 = (f32[1,32,6]{2,1,0:T(8,128)}, f32[1,32,6]{2,1,0:T(8,128)S(1)}, u32[]{:S(2)}) copy-start(f32[1,32,6]{2,1,0:T(8,128)S(1)} %copy.171) | copy-start | bytes 2308
  98.1 23.0 %all-to-all-start.2 = ((bf16[32,2,9,512]{3,1,2,0:T(2,128)(2,1)}), bf16[32,2,9,512]{3,1,2,0:T(2,128)(2,1)S(1)}, u32[]{:S(2)}, u32[]{:S(2)}) async-start(bf16[32,2,9,512]{3,1,2,0:T(2,128)(2,1)} %copy.131), calls=%async_computation.2 | async-start | bytes 1179648 | tf_op jit(solution)/shard_map/all_to_all | solution.py:38
  121.1 22.1 %all-to-all-start.4 = ((bf16[32,2,9,512]{3,1,2,0:T(2,128)(2,1)}), bf16[32,2,9,512]{3,1,2,0:T(2,128)(2,1)S(1)}, u32[]{:S(2)}, u32[]{:S(2)}) async-start(bf16[32,2,9,512]{3,1,2,0:T(2,128)(2,1)} %copy.137), calls=%async_computation.4 | async-start | bytes 1179648 | tf_op jit(solution)/shard_map/all_to_all | solution.py:59
  143.2 4.5 copy-start.3
  143.2 1.8 copy-start.13
  147.7 0.8 copy-start.5
  147.7 1.2 copy-start.9
  150.4 22.4 %all-to-all-start.5 = ((bf16[32,2,9,512]{3,1,2,0:T(2,128)(2,1)}), bf16[32,2,9,512]{3,1,2,0:T(2,128)(2,1)S(1)}, u32[]{:S(2)}, u32[]{:S(2)}) async-start(bf16[32,2,9,512]{3,1,2,0:T(2,128)(2,1)} %copy.139), calls=%async_computation.5 | async-start | bytes 1179648 | tf_op jit(solution)/shard_map/all_to_all | solution.py:72
  159.1 23.9 %copy-start.39 = (s32[64,9,1]{1,0,2:T(8,128)S(1)}, s32[64,9,1]{1,0,2:T(8,128)}, u32[]{:S(2)}) copy-start(s32[64,9,1]{1,0,2:T(8,128)} %get-tuple-element.55) | copy-start | bytes 6916
  172.8 21.1 %all-to-all-start.3 = ((bf16[32,2,9,512]{3,1,2,0:T(2,128)(2,1)}), bf16[32,2,9,512]{3,1,2,0:T(2,128)(2,1)}, u32[]{:S(2)}, u32[]{:S(2)}) async-start(bf16[32,2,9,512]{3,1,2,0:T(2,128)(2,1)} %copy.134), calls=%async_computation.3 | async-start | bytes 1179648 | tf_op jit(solution)/shard_map/all_to_all | solution.py:44
  198.6 4.3 copy-start.43
  200.7 1.4 copy-start.25
  202.0 0.9 copy-start.23
  206.8 1.2 copy-start.35
  208.0 22.7 %copy-start.47 = (f32[32,2,9,352]{3,0,2,1:T(8,128)S(1)}, f32[32,2,9,352]{3,0,2,1:T(8,128)}, u32[]{:S(2)}) copy-start(f32[32,2,9,352]{3,0,2,1:T(8,128)} %get-tuple-element.66) | copy-start | bytes 2433028
  209.5 21.2 %copy-start.16 = (f32[32,2,9,352]{3,0,2,1:T(8,128)S(1)}, f32[32,2,9,352]{3,0,2,1:T(8,128)}, u32[]{:S(2)}) copy-start(f32[32,2,9,352]{3,0,2,1:T(8,128)} %copy-done.15) | copy-start | bytes 2433028
  209.5 21.2 %copy-start.28 = (bf16[2,2,352,512]{3,2,1,0:T(8,128)(2,1)S(1)}, bf16[2,2,352,512]{3,2,1,0:T(8,128)(2,1)}, u32[]{:S(2)}) copy-start(bf16[2,2,352,512]{3,2,1,0:T(8,128)(2,1)} %param.15) | copy-start | bytes 4325380
  229.9 0.8 copy-start.21
  231.4 0.8 copy-start.7
  231.4 2.2 copy-start.10
  231.4 1.7 copy-start.14
  233.6 6.9 %copy-start.6 = (bf16[32,2,9,352]{3,0,2,1:T(8,128)(2,1)S(1)}, bf16[32,2,9,352]{3,0,2,1:T(8,128)(2,1)}, u32[]{:S(2)}) copy-start(bf16[32,2,9,352]{3,0,2,1:T(8,128)(2,1)} %copy-done.5) | copy-start | bytes 1216516
  235.0 20.0 %all-to-all-start.7 = ((bf16[32,2,9,512]{3,1,2,0:T(2,128)(2,1)}), bf16[32,2,9,512]{3,1,2,0:T(2,128)(2,1)S(1)}, u32[]{:S(2)}, u32[]{:S(2)}) async-start(bf16[32,2,9,512]{3,1,2,0:T(2,128)(2,1)} %copy.144), calls=%async_computation.7 | async-start | bytes 1179648 | tf_op jit(solution)/shard_map/all_to_all | solution.py:72
  240.4 4.0 copy-start.4
  240.5 283.5 %all-reduce.5.cloned.1.call-start = ((), (), s32[]{:S(2)}) async-start(), calls=%async_computation.8 | async-start | bytes 2097152 | tf_op jit(solution)/shard_map/psum | solution.py:77
  240.5 3.9 copy-start.46
  244.4 1.5 copy-start.26
  244.4 1.5 copy-start.30
  255.5 1.1 copy-start.33
  255.5 1.3 copy-start.24
  255.5 1.4 copy-start.38
  256.6 1.8 copy-start.8
  258.0 1.8 copy-start.11
  258.0 3.3 copy-start.22
  258.1 3.2 copy-start.45
  258.1 346.1 %all-reduce.7.cloned.1.call-start = ((), (), s32[]{:S(2)}) async-start(), calls=%async_computation.9 | async-start | bytes 8650752 | tf_op jit(solution)/shard_map/psum | solution.py:69
  262.8 0.8 copy-start.31
  262.8 1.5 copy-start.2
  604.2 2.7 copy-start.19
  604.2 2.7 copy-start.20
  606.9 1.3 copy-start.17
  606.9 1.8 copy-start.18
Sparse Core Ops, SparseCore 0:
  258.2 265.7 all-reduce.4
  527.3 76.8 all-reduce.6
where the time goes:
time: 630 us; the launch traced here: 617 us
  waiting for transfers between devices  407 us (65%)
  local copies, waits for them, and re-layouts  69.6 us (11%)
  starting transfers between devices  49.6 us (8%)
  matrix products  28 us (4%)
  other arithmetic  27.5 us (4%)
  blocking collectives  19.7 us (3%)
  between operations  15.5 us (2%)
    psum x1, waiting for transfers between devices, layer_backward(): g_mix = lax.psum(g_mix, ('dp', 'ep'))  259 us
    psum x1, waiting for transfers between devices, layer_backward(): g_gate = lax.psum(g_gate, 'dp')  77.6 us
    all_to_all x2, waiting for transfers between devices, layer_backward(): lax.all_to_all(d_recv, 'ep', 0, 0, tiled=True)  21.7 us
    all_to_all x2, waiting for transfers between devices, layer_forward(): lax.all_to_all(out_buf, 'ep', 0, 0, tiled=True)  19.9 us
    all_to_all x1, blocking collectives, layer_backward(): recv_grad = lax.all_to_all(send_grad, 'ep', 0, 0, tiled=True)  19.7 us
    all_to_all x2, starting transfers between devices, layer_forward(): recv_buf = lax.all_to_all(send_buf, 'ep', 0, 0, tiled=True)  18.4 us
    all_to_all x1, waiting for transfers between devices, layer_backward(): recv_grad = lax.all_to_all(send_grad, 'ep', 0, 0, tiled=True)  15.1 us
    all_to_all x2, starting transfers between devices, layer_forward(): lax.all_to_all(out_buf, 'ep', 0, 0, tiled=True)  14.4 us
  transfers between devices with their start and end apart: 9, of which 8 were waited for; matrix products, arithmetic and copies ran while one was open for 9% of the time, Pallas kernels for 0%

commit v1 on v0

v1 whole, which is shorter than its diff:
```python
import functools

import jax
import jax.numpy as jnp
from jax import lax
from jax.experimental import pallas as pl
from jax.experimental.pallas import tpu as pltpu
from jax.sharding import PartitionSpec as P

NZ, NY, NX = 8, 4, 4
T = 32
D = 512
FF, FP = 352, 384
GR = 3 * FF
HR = GR // 2
NT = NZ * NY * T
CH = NY * T
SL = D // (NZ * NY)
BF, F32 = jnp.bfloat16, jnp.float32
MESH = pl.DeviceIdType.MESH
PLUS, MINUS = 0, 1
SIGN = (1, -1)
LANES = 128
ZSEM = (2, 4, 4)


def vmem(dims, dtype=BF):
    return pltpu.VMEM(dims, dtype)


def both(*dims):
    return (2, 2, *dims)


def dot(a, b, ca=1, cb=0):
    return lax.dot_general(a, b, (((ca,), (cb,)), ((), ())), preferred_element_type=F32)


def dot_nt(a, b):
    return dot(a, b, 1, 1)


def dot_tn(a, b):
    return dot(a, b, 0, 0)


def lim(direction, unit):
    return 4 if (unit < 2) == (direction == PLUS) else 3


def step_kernel(tok, dout, ids, gates, wmix, wg_hbm, wu_hbm, wd_hbm,
                y_out, dx_out, dmix_out, dg_out, du_out, dw_out,
                w3, x1, x2, dyg, du2, du1, u1, u2, gt, ab, hb, dab, cb_, pacc, pacc2,
                rs_first, rs_recv, rs_fin, rs_ys, rs_yr,
                grad, rd, rg, fin,
                dm_full, dm_send, dm_recv, dm_all,
                w_sem, ag_ys, ag_yr, ag_zs, ag_zr, rs_s, rs_r, rs_ysm, rs_yrm,
                ar_s, ar_r, dx_s, dx_r, out_sem, dy_s, dy_r):
    ep = lax.axis_index('ep')
    dp = lax.axis_index('dp')
    z, y = lax.div(ep, NY), lax.rem(ep, NY)
    x, core = lax.div(dp, 2), lax.rem(dp, 2)

    z_at = [lax.rem(z + i, NZ) for i in range(NZ)]
    y_at = [lax.rem(y + i, NY) for i in range(NY)]
    x_at = [lax.rem(x + i, NX) for i in range(NX)]
    ep_at = [[zz * NY + yy for yy in y_at] for zz in z_at]
    rows_at = {rows: [[pl.multiple_of(v * rows, rows) for v in line] for line in ep_at] for rows in (T, SL)}
    plane_at = [zz * NY for zz in z_at]
    home_at = [[pl.multiple_of((zz + yd) * T, T) for yd in range(NY)] for zz in plane_at]
    unit_at = [pl.multiple_of(yy * T, T) for yy in y_at]
    dp_x = [xx * 2 + core for xx in x_at]
    dp_r = [lax.rem(dp + r, 8) for r in range(8)]
    partner = dp + 1 - 2 * core
    q128 = [pl.multiple_of(xx * 128, 128) for xx in x_at]
    q64 = [[pl.multiple_of(xx * 128 + 64 * h, 64) for h in range(2)] for xx in x_at]

    def ep_of(dz, dy):
        return ep_at[dz % NZ][dy % NY]

    def dp_of(dx):
        return dp_x[dx % NX]

    def remote(src, dst, ssem, rsem, ep_to=None, dp_to=None):
        return pltpu.make_async_remote_copy(
            src_ref=src, dst_ref=dst, send_sem=ssem, recv_sem=rsem,
            device_id=(ep if ep_to is None else ep_to, dp if dp_to is None else dp_to),
            device_id_type=MESH)

    barrier = pltpu.get_barrier_semaphore()
    peers = [(ep_of(0, j), dp) for j in range(1, NY)]
    peers += [(ep_of(1, 0), dp), (ep_of(-1, 0), dp)]
    peers += [(ep, dp_r[r]) for r in range(1, 8)]
    for peer in peers:
        pl.semaphore_signal(barrier, inc=1, device_id=peer, device_id_type=MESH)

    loads = []
    for p, src in enumerate((wg_hbm, wu_hbm, wd_hbm)):
        for l in range(2):
            for e in range(2):
                loads.append(pltpu.make_async_copy(src.at[l, e], w3.at[l, e, pl.ds(FP * p, FF), :],
                                                   w_sem.at[p, l, e]))
    for load in loads:
        load.start()

    class Gather:
        def __init__(self, view, s, r):
            self.view, self.s, self.r = view, s, r

        def block(self, dz, dy):
            return self.view(dz % NZ, dy % NY)

        def ycopy(self, j, from_j):
            blk = self.block(0, -from_j)
            return remote(blk, blk, ag_ys.at[self.s, j - 1], ag_yr.at[self.r, j - 1], ep_to=ep_of(0, j))

        def zcopy(self, direction, dist, j, arriving):
            sign = SIGN[direction]
            blk = self.block(-sign * (dist if arriving else dist - 1), -j)
            return remote(blk, blk, ag_zs.at[self.s, direction, dist - 1, j],
                          ag_zr.at[self.r, direction, dist - 1, j], ep_to=ep_of(sign, 0))

        def start(self):
            for direction in (PLUS, MINUS):
                self.zcopy(direction, 1, 0, False).start()
            for j in range(1, NY):
                self.ycopy(j, 0).start()

        def y_arrive(self):
            for j in (1, 3, 2):
                self.ycopy(j, j).wait_recv()
                for direction in (PLUS, MINUS):
                    self.zcopy(direction, 1, j, False).start()

        def poll(self, p):
            dist = p // 2 + 1
            for j in (2 * (p % 2), 2 * (p % 2) + 1):
                for direction in (PLUS, MINUS):
                    if dist <= lim(direction, j):
                        self.zcopy(direction, dist, j, True).wait_recv()
                        if dist < lim(direction, j):
                            self.zcopy(direction, dist + 1, j, False).start()

        def chunk(self, k):
            if k == 0:
                self.y_arrive()
            elif k == 1:
                self.poll(0)
            if k > 0:
                self.poll(k)

        def drain(self):
            for j in range(1, NY):
                self.ycopy(j, 0).wait_send()
            for direction in (PLUS, MINUS):
                for j in range(NY):
                    for dist in range(1, lim(direction, j) + 1):
                        self.zcopy(direction, dist, j, False).wait_send()

    class ColumnGather:
        def zcopy(self, direction, dist, arriving):
            sign = SIGN[direction]
            zz = z_at[(-sign * (dist if arriving else dist - 1)) % NZ]
            blk = dyg.at[zz, pl.ds(unit_at[0], T), :]
            return remote(blk, blk, dy_s.at[direction, dist - 1], dy_r.at[direction, dist - 1], ep_to=ep_of(sign, 0))

        def ycopy(self, direction, hop, arriving):
            sign = SIGN[direction]
            col = unit_at[(-sign * (hop if arriving else hop - 1)) % NY]
            planes = pl.ds(0, NZ) if hop == 1 else pl.ds(4 * direction, 4)
            blk = dyg.at[planes, pl.ds(col, T), :]
            return remote(blk, blk, dy_s.at[direction, 3 + hop], dy_r.at[direction, 3 + hop], ep_to=ep_of(0, sign))

        def start(self):
            for direction in (PLUS, MINUS):
                self.zcopy(direction, 1, False).start()

        def zpoll(self, dist):
            for direction in (PLUS, MINUS):
                if dist <= 4 - direction:
                    self.zcopy(direction, dist, True).wait_recv()
                    if dist < 4 - direction:
                        self.zcopy(direction, dist + 1, False).start()
            if dist == 4:
                for direction in (PLUS, MINUS):
                    self.ycopy(direction, 1, False).start()

        def ypoll(self, hop):
            for direction in (PLUS, MINUS):
                self.ycopy(direction, hop, True).wait_recv()
                if hop == 1:
                    self.ycopy(direction, 2, False).start()

        def drain(self):
            for direction in (PLUS, MINUS):
                for dist in range(1, 5 - direction):
                    self.zcopy(direction, dist, False).wait_send()
                for hop in (1, 2):
                    self.ycopy(direction, hop, False).wait_send()

    class Scatter:
        def __init__(self, part, n):
            self.part, self.n = part, n

        def rows(self, dz, yd):
            return pl.ds(home_at[dz % NZ][yd], T)

        def zcopy(self, direction, s, yd):
            sign = SIGN[direction]
            unit = pl.ds(yd * T, T)
            n = self.n
            src = rs_first.at[n, direction, unit, :] if s == 0 else rs_recv.at[n, direction, s - 1, unit, :]
            last = s == lim(direction, yd) - 1
            dst = rs_fin.at[n, direction, unit, :] if last else rs_recv.at[n, direction, s, unit, :]
            return remote(src, dst, rs_s.at[n // 3, direction, s, yd], rs_r.at[n, direction, s, yd], ep_to=ep_of(sign, 0))

        def round(self, s):
            for yd in range(NY):
                for direction in (PLUS, MINUS):
                    hops = lim(direction, yd)
                    sign = SIGN[direction]
                    if s > hops:
                        continue
                    if s > 0:
                        self.zcopy(direction, s - 1, yd).wait_recv()
                    if s == hops:
                        continue
                    unit = pl.ds(yd * T, T)
                    mine = self.part[self.rows(sign * (hops - s), yd), :]
                    if s == 0:
                        rs_first[self.n, direction, unit, :] = mine.astype(BF)
                    else:
                        got = rs_recv[self.n, direction, s - 1, unit, :]
                        rs_recv[self.n, direction, s - 1, unit, :] = (mine + got.astype(F32)).astype(BF)
                    self.zcopy(direction, s, yd).start()

        def plane(self, dy):
            unit = pl.ds(unit_at[dy % NY], T)
            return (self.part[pl.ds(rows_at[T][0][dy % NY], T), :] + rs_fin[self.n, PLUS, unit, :].astype(F32)
                    + rs_fin[self.n, MINUS, unit, :].astype(F32))

        def ycopy(self, j):
            return remote(rs_ys.at[self.n, j - 1], rs_yr.at[self.n, j - 1], rs_ysm.at[self.n // 3, j - 1],
                          rs_yrm.at[self.n, j - 1], ep_to=ep_of(0, j))

        def y_start(self):
            for j in range(1, NY):
                rs_ys[self.n, j - 1] = self.plane(j).astype(BF)
                self.ycopy(j).start()

        def finish(self):
            total = self.plane(0)
            for j in range(1, NY):
                self.ycopy(j).wait_recv()
                total = total + rs_yr[self.n, j - 1].astype(F32)
            for yd in range(NY):
                for direction in (PLUS, MINUS):
                    for s in range(lim(direction, yd)):
                        self.zcopy(direction, s, yd).wait_send()
            for j in range(1, NY):
                self.ycopy(j).wait_send()
            return total

    class Reduce:
        def __init__(self, n):
            self.n = n

        def copy(self, src, dst, slot, dp_to):
            return remote(src, dst, ar_s.at[self.n, slot], ar_r.at[self.n, slot], dp_to=dp_to)

        def swap(self):
            n = self.n
            return self.copy(grad.at[n, 1 - core, pl.ds(0, GR), :], rd.at[n], 0, partner)

        def part(self, q, h):
            return rd.at[self.n, pl.ds(HR * h, HR), pl.ds(q128[q % NX], LANES)]

        def slot(self, i):
            return rg.at[self.n, i]

        def scatter_copy(self, i):
            right, left = dp_of(1), dp_of(-1)
            src = self.slot(i - 4) if i >= 4 else self.part(*((2, 0), (-2, 1), (-1, 0), (1, 1))[i])
            to = [right, left, left, right, right, left][i]
            return self.copy(src, self.slot(i), 1 + i, to)

        def fin(self, q, h=None):
            rows = pl.ds(0, GR) if h is None else pl.ds(HR * h, HR)
            return fin.at[self.n, core, rows, pl.ds(q128[q % NX], LANES)]

        def gather_copy(self, i, arriving=False):
            right, left = dp_of(1), dp_of(-1)
            sent = [(0, None), (0, None), (-1, 0), (1, 1)][i]
            came = [(-1, None), (1, None), (-2, 0), (2, 1)][i]
            ref = self.fin(*(came if arriving else sent))
            return self.copy(ref, ref, 7 + i, [right, left, right, left][i])

        def back(self, arriving=False):
            ref = fin.at[self.n, 1 - core if arriving else core]
            return self.copy(ref, ref, 11, partner)

        def out(self):
            return [pltpu.make_async_copy(fin.at[self.n, e, pl.ds(FF * p, FF), :], dst.at[self.n, e],
                                          out_sem.at[self.n, e, p])
                    for e in range(2) for p, dst in enumerate((dg_out, du_out, dw_out))]

        def stage(self, i):
            n = self.n
            if i == 0:
                self.swap().start()
            elif i == 1:
                self.swap().wait_recv()

                @pl.loop(0, 3)
                def _(r):
                    rows = pl.ds(pl.multiple_of(r * FF, FF), FF)
                    rd[n, rows, :] = (rd[n, rows, :].astype(F32) + grad[n, core, rows, :].astype(F32)).astype(BF)

                for i2 in range(4):
                    self.scatter_copy(i2).start()
            elif i == 2:
                for i2, q, h in ((0, 1, 0), (1, -1, 1)):
                    self.scatter_copy(i2).wait_recv()
                    got = self.slot(i2)
                    got[...] = (got[...].astype(F32) + self.part(q, h)[...].astype(F32)).astype(BF)
                    self.scatter_copy(4 + i2).start()
            elif i == 3:
                for i2 in (2, 3, 4, 5):
                    self.scatter_copy(i2).wait_recv()
                for h in range(2):
                    self.fin(0, h)[...] = (self.part(0, h)[...].astype(F32) + self.slot(2 + h)[...].astype(F32)
                                           + self.slot(4 + h)[...].astype(F32)).astype(BF)
                self.gather_copy(0).start()
                self.gather_copy(1).start()
            elif i == 4:
                for i2 in range(2):
                    self.gather_copy(i2, True).wait_recv()
                    self.gather_copy(2 + i2).start()
            elif i == 5:
                self.gather_copy(2, True).wait_recv()
                self.gather_copy(3, True).wait_recv()
                self.back().start()
            elif i == 6:
                self.back(True).wait_recv()
                for c in self.out():
                    c.start()
                for i2 in range(6):
                    self.scatter_copy(i2).wait_send()
                for i2 in range(4):
                    self.gather_copy(i2).wait_send()
                self.swap().wait_send()
                self.back().wait_send()
            elif i == 7:
                for c in self.out():
                    c.wait()

    slice_rows = pl.ds(pl.multiple_of(lax.rem(ep, 8) * SL, SL), SL)

    def mix_copy(n, r):
        return remote(dm_send.at[n], dm_recv.at[n, r - 1], dx_s.at[n, r - 1], dx_r.at[n, r - 1], dp_to=dp_r[r])

    def mix_start(n, xg, dug):
        lanes = pl.ds(pl.multiple_of(lax.div(ep, 8) * 128, 128), 128)
        dm_full[n] = dot_tn(xg[:, lanes], dug[...])
        dm_send[n] = dm_full[n, slice_rows, :].astype(BF)
        for r in range(1, 8):
            mix_copy(n, r).start()

    def mix_sum(n):
        own = pl.ds(rows_at[SL][0][0], SL)
        total = dm_full[n, slice_rows, :]
        for r in range(1, 8):
            mix_copy(n, r).wait_recv()
            total = total + dm_recv[n, r - 1].astype(F32)
        dm_all[n, own, :] = total.astype(BF)
        for r in range(1, 8):
            mix_copy(n, r).wait_send()

    own_rows = pl.ds(rows_at[T][0][0], T)
    home_unit = pl.ds(unit_at[0], T)

    def plane_rows(k):
        return pl.ds(pl.multiple_of(plane_of(k) * CH, CH), CH)

    def plane_of(k):
        odd = lax.rem(k, 2)
        dist = lax.div(k + 1, 2)
        return lax.rem(z + NZ - odd * dist + (1 - odd) * dist, NZ)

    def gate_col(layer, e, rows):
        table = gt[rows, :]
        lane = lax.broadcasted_iota(jnp.int32, (CH, 128), 1)
        return jnp.sum(jnp.where(lane == layer * 64 + ep * 2 + e, table, 0.0), axis=1, keepdims=True)

    def expert_in(u, gcol):
        return jnp.where(gcol > 0.0, u, 0.0).astype(BF)

    x1[own_rows, :] = tok[...]
    slot = lax.broadcasted_iota(jnp.int32, (LANES, T), 0)
    table = jnp.zeros((LANES, T), F32)
    for l in range(2):
        for j in range(6):
            table = table + jnp.where(slot == ids[j, l:l + 1, :] + 64 * l, gates[j, l:l + 1, :], 0.0)
    gt[own_rows, :] = table.T
    dyg[z, home_unit, :] = dout[...]
    pl.semaphore_wait(barrier, len(peers))

    def row_view(buf):
        return lambda dz, dy: buf.at[pl.ds(rows_at[T][dz][dy], T), :]

    ag_tok = Gather(row_view(x1), 0, 0)
    ag_gt = Gather(row_view(gt), 1, 1)
    ag_dy = ColumnGather()
    ag_x2 = Gather(row_view(x2), 0, 2)
    ag_du2 = Gather(row_view(du2), 1, 3)
    ag_du1 = Gather(row_view(du1), 0, 4)
    ag_mix = Gather(lambda dz, dy: dm_all.at[:, pl.ds(rows_at[SL][dz][dy], SL), :], 1, 5)
    ag_tok.start()
    ag_gt.start()
    ag_dy.start()

    for load in loads:
        load.wait()
    for l in range(2):
        for e in range(2):
            for p in range(3):
                w3[l, e, FP * p + FF:FP * p + FP, :] = jnp.zeros((FP - FF, D), BF)

    def gate_up(l, e):
        return w3[l, e, 0:2 * FP, :]

    def down(l, e):
        return w3[l, e, 2 * FP:, :]

    @pl.loop(0, 8)
    def _(k):
        for kk in range(8):
            @pl.when(k == kk)
            def _(kk=kk):
                ag_tok.chunk(kk)
                ag_gt.chunk(kk)
                if kk in (1, 3, 5, 7):
                    ag_dy.zpoll((kk + 1) // 2)
        rows = plane_rows(k)
        xc = x1[rows, :]
        u = (xc.astype(F32) + dot(xc, wmix[0])).astype(BF)
        u1[rows, :] = u
        uf = u.astype(F32)
        total = jnp.zeros((CH, D), F32)
        for e in range(2):
            gcol = gate_col(0, e, rows)
            pre = dot_nt(expert_in(uf, gcol), gate_up(0, e))
            ab[e, rows, :] = pre
            a, b = pre[:, :FP], pre[:, FP:]
            h = (a * jax.nn.sigmoid(a) * b).astype(BF)
            hb[0, e, rows, :] = h
            total = total + gcol * dot(h, down(0, e)).astype(BF).astype(F32)
        pacc[rows, :] = total

    rs = Scatter(pacc, 0)
    for s in range(5):
        rs.round(s)
        if s in (2, 4):
            ag_dy.ypoll(s // 2)
    rs.y_start()
    ag_tok.drain()
    ag_gt.drain()
    ag_dy.drain()
    y1 = (u1[own_rows, :].astype(F32) + rs.finish()).astype(BF)
    x2[own_rows, :] = y1
    ag_x2.start()

    def backward_part(layer, e, rows, gcol, dyc, pre):
        a, b = pre[:, :FP], pre[:, FP:]
        c = (gcol * dyc).astype(BF)
        cb_[e, rows, :] = c
        dh = dot_nt(c, down(layer, e))
        s = jax.nn.sigmoid(a)
        dab[e, rows, 0:FP] = (dh * b * (s * (1.0 + a * (1.0 - s)))).astype(BF)
        dab[e, rows, FP:] = (dh * (a * s)).astype(BF)
        v = dot(dab[e, rows, :], gate_up(layer, e)).astype(BF)
        return gcol * v.astype(F32)

    @pl.loop(0, 8)
    def _(k):
        for kk in range(8):
            @pl.when(k == kk)
            def _(kk=kk):
                ag_x2.chunk(kk)
        rows = plane_rows(k)
        xc = x2[rows, :]
        u = (xc.astype(F32) + dot(xc, wmix[1])).astype(BF)
        u2[rows, :] = u
        uf = u.astype(F32)
        dyc = dyg[plane_of(k)].astype(F32)
        total = jnp.zeros((CH, D), F32)
        back = jnp.zeros((CH, D), F32)
        for e in range(2):
            gcol = gate_col(1, e, rows)
            pre = dot_nt(expert_in(uf, gcol), gate_up(1, e))
            a, b = pre[:, :FP], pre[:, FP:]
            h = (a * jax.nn.sigmoid(a) * b).astype(BF)
            hb[1, e, rows, :] = h
            total = total + gcol * dot(h, down(1, e)).astype(BF).astype(F32)
            back = back + backward_part(1, e, rows, gcol, dyc, pre)
        pacc2[rows, :] = total
        pacc[rows, :] = back

    def weight_grads(layer, e, ug):
        @pl.loop(0, 6)
        def _(i):
            part = lax.div(i, 3)
            cols = pl.ds(pl.multiple_of(i * LANES, LANES), LANES)
            rows = pl.ds(pl.multiple_of(part * FF + (i - 3 * part) * LANES, 32), LANES)
            grad[layer, e, rows, :] = dot_tn(dab[e, :, cols], ug[...]).astype(BF)

        @pl.loop(0, 3)
        def _(i):
            cols = pl.ds(pl.multiple_of(i * LANES, LANES), LANES)
            rows = pl.ds(pl.multiple_of(2 * FF + i * LANES, 32), LANES)
            grad[layer, e, rows, :] = dot_tn(hb[layer, e, :, cols], cb_[e]).astype(BF)

    rs = Scatter(pacc, 1)
    rs.round(0)
    weight_grads(1, 0, u2)
    rs.round(1)
    weight_grads(1, 1, u2)
    ar2 = Reduce(1)
    ar2.stage(0)
    for s in range(2, 5):
        rs.round(s)
    rs.y_start()
    ag_x2.drain()
    du2[own_rows, :] = (dout[...].astype(F32) + rs.finish()).astype(BF)
    ag_du2.start()
    ar2.stage(1)

    rs_y2 = Scatter(pacc2, 3)

    @pl.loop(0, 8)
    def _(k):
        for kk in range(8):
            @pl.when(k == kk)
            def _(kk=kk):
                ag_du2.chunk(kk)
                if kk in (2, 5):
                    rs_y2.round(kk // 3)
                if kk == 4:
                    ar2.stage(2)
        rows = plane_rows(k)
        duc = du2[rows, :]
        dyc = (duc.astype(F32) + dot_nt(duc, wmix[1])).astype(BF)
        dyg[plane_of(k)] = dyc
        dyc = dyc.astype(F32)
        back = jnp.zeros((CH, D), F32)
        for e in range(2):
            back = back + backward_part(0, e, rows, gate_col(0, e, rows), dyc, ab[e, rows, :])
        pacc[rows, :] = back

    rs = Scatter(pacc, 2)
    rs.round(0)
    ar2.stage(3)
    weight_grads(0, 0, u1)
    rs.round(1)
    weight_grads(0, 1, u1)
    ar1 = Reduce(0)
    ar1.stage(0)
    rs_y2.round(2)
    rs.round(2)
    mix_start(1, x2, du2)
    ar1.stage(1)
    rs.round(3)
    ar2.stage(4)
    rs_y2.round(3)
    rs.round(4)
    rs.y_start()
    ag_du2.drain()
    mix_sum(1)
    d_u1 = (dyg[z, home_unit, :].astype(F32) + rs.finish()).astype(BF)
    du1[own_rows, :] = d_u1
    ag_du1.start()
    dx_out[...] = (d_u1.astype(F32) + dot_nt(d_u1, wmix[0])).astype(BF)

    rs_y2.round(4)
    rs_y2.y_start()
    ag_du1.chunk(0)
    ar2.stage(5)
    for k in range(1, 4):
        ag_du1.chunk(k)
    ar1.stage(2)
    for k in range(4, 6):
        ag_du1.chunk(k)
    ar2.stage(6)
    for k in range(6, 8):
        ag_du1.chunk(k)
    mix_start(0, x1, du1)
    y_out[...] = (u2[own_rows, :].astype(F32) + rs_y2.finish()).astype(BF)
    ar1.stage(3)
    mix_sum(0)
    ag_mix.start()
    for k in range(3):
        ag_mix.chunk(k)
    ar1.stage(4)
    for k in range(3, 6):
        ag_mix.chunk(k)
    ar1.stage(5)
    for k in range(6, 8):
        ag_mix.chunk(k)
    dmix_out[...] = dm_all[...]
    ar1.stage(6)
    ar2.stage(7)
    ar1.stage(7)
    ag_du1.drain()
    ag_mix.drain()


def copy_kernel(*refs):
    n = len(refs) // 3
    src, dst, buf, sem = refs[:n], refs[n:2 * n], refs[2 * n:3 * n], refs[3 * n]
    loads = [pltpu.make_async_copy(src[i], buf[i], sem.at[0, i]) for i in range(n)]
    stores = [pltpu.make_async_copy(buf[i], dst[i], sem.at[1, i]) for i in range(n)]
    for load in loads:
        load.start()
    for load, store in zip(loads, stores):
        load.wait()
        store.start()
    for store in stores:
        store.wait()


def solution(mesh):
    tok_spec = P(('dp', 'ep'))
    route_spec = P(None, ('dp', 'ep'))
    whole_spec = P()
    expert_spec = P(None, 'ep')

    def device_step(tokens, d_out, expert_ids, gate_vals, w_mix, w_gate, w_up, w_down):
        vm = pl.BlockSpec(memory_space=pltpu.VMEM)
        hbm = pl.BlockSpec(memory_space=pl.ANY)
        shape = jax.ShapeDtypeStruct
        dma = pltpu.SemaphoreType.DMA
        wg_t, wu_t = jnp.swapaxes(w_gate, 2, 3), jnp.swapaxes(w_up, 2, 3)
        results = pl.pallas_call(
            step_kernel,
            out_shape=(shape((T, D), BF), shape((T, D), BF), shape((2, D, D), BF),
                       *[shape(both(FF, D), BF)] * 3),
            in_specs=[vm] * 5 + [hbm] * 3,
            out_specs=(vm,) * 3 + (hbm,) * 3,
            scratch_shapes=[
                vmem(both(3 * FP, D)),
                *[vmem((NT, D))] * 2, vmem((NZ, CH, D)), *[vmem((NT, D))] * 4,
                vmem((NT, LANES), F32), vmem((2, NT, 2 * FP), F32),
                vmem(both(NT, FP)), vmem((2, NT, 2 * FP)), vmem((2, NT, D)),
                vmem((NT, D), F32), vmem((NT, D), F32),
                vmem((4, 2, CH, D)), vmem((4, 2, 3, CH, D)), vmem((4, 2, CH, D)),
                vmem((4, 3, T, D)), vmem((4, 3, T, D)),
                vmem(both(GR + 32, D)), vmem((2, GR, D)), vmem((2, 6, HR, LANES)), vmem(both(GR, D)),
                vmem((2, LANES, D), F32), vmem((2, SL, D)), vmem((2, 7, SL, D)), vmem((2, D, D)),
                dma((3, 2, 2)),
                dma((2, 3)), dma((6, 3)), dma((2, *ZSEM)), dma((6, *ZSEM)),
                dma((2, *ZSEM)), dma((4, *ZSEM)), dma((2, 3)), dma((4, 3)),
                dma((2, 12)), dma((2, 12)), dma((2, 7)), dma((2, 7)), dma((2, 2, 3)), dma((2, 6)), dma((2, 6)),
            ],
            compiler_params=pltpu.CompilerParams(
                collective_id=0, has_side_effects=True, vmem_limit_bytes=67043328),
        )(tokens, d_out, jnp.transpose(expert_ids, (2, 0, 1)), jnp.transpose(gate_vals, (2, 0, 1)),
          w_mix, wg_t, wu_t, w_down)
        y, dx, dmix, dg_t, du_t, dw = pl.pallas_call(
            copy_kernel,
            out_shape=[shape(r.shape, r.dtype) for r in results],
            in_specs=[hbm] * 6,
            out_specs=[hbm] * 6,
            scratch_shapes=[vmem(r.shape) for r in results] + [dma((2, 6))],
        )(*results)
        return y, dx, dmix, jnp.swapaxes(dg_t, 2, 3), jnp.swapaxes(du_t, 2, 3), dw

    return jax.shard_map(device_step, mesh=mesh,
                         in_specs=(tok_spec, tok_spec, route_spec, route_spec, whole_spec,
                                   expert_spec, expert_spec, expert_spec),
                         out_specs=(tok_spec, tok_spec, whole_spec, expert_spec, expert_spec, expert_spec),
                         check_vma=False)
```

time: 630 us -> 196 us (0.31); the launches traced: 617 us -> 196 us
  waiting for transfers between devices: 407 us -> 0 us
  Pallas kernels: 0 us -> 195 us
  local copies, waits for them, and re-layouts: 69.6 us -> 0 us
  starting transfers between devices: 49.6 us -> 0 us
  matrix products: 28 us -> 0 us
  other arithmetic: 27.5 us -> 0 us
  blocking collectives: 19.7 us -> 0 us
  between operations: 15.5 us -> 0.64 us
    psum x2 -> x0, waiting for transfers between devices: 336 us -> none  [the longest x1 259 us: layer_backward(): g_mix = lax.psum(g_mix, ('dp', 'ep'))]
    pallas_call x0 -> x2, Pallas kernels: none -> 195 us  [the longest x1 190 us: device_step(): pl.pallas_call(step_kernel, out_shape=(shape((T, D), BF), shape((T, D), B...]
    all_to_all x7 -> x0, waiting for transfers between devices: 70.7 us -> none  [the longest x2 21.7 us: layer_backward(): lax.all_to_all(d_recv, 'ep', 0, 0, tiled=True)]
    all_to_all x7 -> x0, starting transfers between devices: 49.3 us -> none  [the longest x2 18.4 us: layer_forward(): recv_buf = lax.all_to_all(send_buf, 'ep', 0, 0, tiled=True)]
    gather x20 -> x0, local copies, waits for them, and re-layouts: 33.3 us -> none  [the longest x4 8.12 us: route_tables(): sort_order[jnp.minimum(starts[:, None] + slot_pos[None, :], n_copies - 1)]]
    dot_general x24 -> x0, matrix products: 28 us -> none  [the longest x2 4.04 us: layer_forward(): jnp.einsum('secd,edf->secf', recv_buf, w_up, preferred_element_type=jnp.f...]
    all_to_all x1 -> x0, blocking collectives: 19.7 us -> none  [layer_backward(): recv_grad = lax.all_to_all(send_grad, 'ep', 0, 0, tiled=True)]
    select_n x10 -> x0, local copies, waits for them, and re-layouts: 7.12 us -> none  [the longest x2 3.4 us: layer_backward(): jnp.where(is_valid[:, :, None], g_dy[src_copy], 0).reshape(recv_buf.shape)]
  transfers between devices with their start and end apart: 9 -> 0, of which waited for: 8 -> 0; matrix products, arithmetic and copies ran while one was open for 9% -> 0% of each run, Pallas kernels for 0% -> 0%
where the time goes in v1:
time: 196 us
  Pallas kernels  195 us (99%)
    pallas_call x1, Pallas kernels, device_step(): pl.pallas_call(step_kernel, out_shape=(shape((T, D), BF), shape((T, D), B...  190 us
    pallas_call x1, Pallas kernels, device_step(): pl.pallas_call(copy_kernel, out_shape=[shape(r.shape, r.dtype) for r in r...  4.76 us

profile of v1, /device:TPU:1, one launch (start us, length us, event | category | flops | bytes accessed | tf_op | source)
XLA Modules:
  0.0 195.8 jit_solution(10279749502912586578)
XLA Ops:
  0.6 190.4 %shard_map.127 = (bf16[32,512]{1,0:T(8,128)(2,1)}, bf16[32,512]{1,0:T(8,128)(2,1)}, bf16[2,512,512]{2,1,0:T(8,128)(2,1)}, bf16[2,2,352,512]{3,2,1,0:T(8,128)(2,1...) custom-call(bf16[32,512]{1,0:T(8,128)(2,1)} %tok.1, bf16[32,512]{1,0:T(8,128)(2,1)} %dout.1, ...), custom_call_target="tpu_custom_call" | custom-call | tf_op jit(solution)/shard_map/pallas_call | solution.py:643
  191.0 4.8 %shard_map.128 = (bf16[32,512]{1,0:T(8,128)(2,1)}, bf16[32,512]{1,0:T(8,128)(2,1)}, bf16[2,512,512]{2,1,0:T(8,128)(2,1)}, bf16[2,2,352,512]{3,2,1,0:T(8,128)(2,1...) custom-call(bf16[32,512]{1,0:T(8,128)(2,1)} %get-tuple-element.18.refs_0_, ...), custom_call_target="tpu_custom_call" | custom-call | tf_op jit(solution)/shard_map/pallas_call | solution.py:668

commit v2 on v1

--- a/solution.py
+++ b/solution.py
@@ -13,9 +13,10 @@
 FF, FP = 352, 384
 GR = 3 * FF
 HR = GR // 2
-NT = NZ * NY * T
+NEP, NDP = NZ * NY, 2 * NX
+NT = NEP * T
 CH = NY * T
-SL = D // (NZ * NY)
+SL = D // NEP
 BF, F32 = jnp.bfloat16, jnp.float32
 MESH = pl.DeviceIdType.MESH
 PLUS, MINUS = 0, 1
@@ -53,9 +54,10 @@
                 w3, x1, x2, dyg, du2, du1, u1, u2, gt, ab, hb, dab, cb_, pacc, pacc2,
                 rs_first, rs_recv, rs_fin, rs_ys, rs_yr,
                 grad, rd, rg, fin,
-                dm_full, dm_send, dm_recv, dm_all,
+                dm_full, dm_own, dm_send, dm_recv, dm_all, dm_part, dm_mid, dm_y, dm_z,
                 w_sem, ag_ys, ag_yr, ag_zs, ag_zr, rs_s, rs_r, rs_ysm, rs_yrm,
-                ar_s, ar_r, dx_s, dx_r, out_sem, dy_s, dy_r):
+                ar_s, ar_r, dx_s, dx_r, out_sem, dy_s, dy_r,
+                mg_s, mg_r, ms_s, ms_r):
     ep = lax.axis_index('ep')
     dp = lax.axis_index('dp')
     z, y = lax.div(ep, NY), lax.rem(ep, NY)
@@ -88,11 +90,13 @@
             device_id_type=MESH)
 
     barrier = pltpu.get_barrier_semaphore()
-    peers = [(ep_of(0, j), dp) for j in range(1, NY)]
-    peers += [(ep_of(1, 0), dp), (ep_of(-1, 0), dp)]
-    peers += [(ep, dp_r[r]) for r in range(1, 8)]
-    for peer in peers:
-        pl.semaphore_signal(barrier, inc=1, device_id=peer, device_id_type=MESH)
+
+    @pl.loop(1, NEP)
+    def _(r):
+        pl.semaphore_signal(barrier, inc=1, device_id=(lax.rem(ep + r, NEP), dp), device_id_type=MESH)
+
+    for r in range(1, NDP):
+        pl.semaphore_signal(barrier, inc=1, device_id=(ep, dp_r[r]), device_id_type=MESH)
 
     loads = []
     for p, src in enumerate((wg_hbm, wu_hbm, wd_hbm)):
@@ -253,13 +257,15 @@
             for j in range(1, NY):
                 self.ycopy(j).wait_recv()
                 total = total + rs_yr[self.n, j - 1].astype(F32)
+            return total
+
+        def drain(self):
             for yd in range(NY):
                 for direction in (PLUS, MINUS):
                     for s in range(lim(direction, yd)):
                         self.zcopy(direction, s, yd).wait_send()
             for j in range(1, NY):
                 self.ycopy(j).wait_send()
-            return total
 
     class Reduce:
         def __init__(self, n):
@@ -290,8 +296,8 @@
 
         def gather_copy(self, i, arriving=False):
             right, left = dp_of(1), dp_of(-1)
-            sent = [(0, None), (0, None), (-1, 0), (1, 1)][i]
-            came = [(-1, None), (1, None), (-2, 0), (2, 1)][i]
+            sent = [(0,), (0,), (-1, 0), (1, 1)][i]
+            came = [(-1,), (1,), (-2, 0), (2, 1)][i]
             ref = self.fin(*(came if arriving else sent))
             return self.copy(ref, ref, 7 + i, [right, left, right, left][i])
 
@@ -319,13 +325,13 @@
                 for i2 in range(4):
                     self.scatter_copy(i2).start()
             elif i == 2:
-                for i2, q, h in ((0, 1, 0), (1, -1, 1)):
+                for i2 in range(2):
                     self.scatter_copy(i2).wait_recv()
                     got = self.slot(i2)
-                    got[...] = (got[...].astype(F32) + self.part(q, h)[...].astype(F32)).astype(BF)
+                    got[...] = (got[...].astype(F32) + self.part(SIGN[i2], i2)[...].astype(F32)).astype(BF)
                     self.scatter_copy(4 + i2).start()
             elif i == 3:
-                for i2 in (2, 3, 4, 5):
+                for i2 in range(2, 6):
                     self.scatter_copy(i2).wait_recv()
                 for h in range(2):
                     self.fin(0, h)[...] = (self.part(0, h)[...].astype(F32) + self.slot(2 + h)[...].astype(F32)
@@ -359,23 +365,112 @@
     def mix_copy(n, r):
         return remote(dm_send.at[n], dm_recv.at[n, r - 1], dx_s.at[n, r - 1], dx_r.at[n, r - 1], dp_to=dp_r[r])
 
+    def mix_send(n):
+        dm_send[n] = dm_own[n].astype(BF)
+        for r in range(1, NDP):
+            mix_copy(n, r).start()
+
     def mix_start(n, xg, dug):
-        lanes = pl.ds(pl.multiple_of(lax.div(ep, 8) * 128, 128), 128)
-        dm_full[n] = dot_tn(xg[:, lanes], dug[...])
-        dm_send[n] = dm_full[n, slice_rows, :].astype(BF)
-        for r in range(1, 8):
-            mix_copy(n, r).start()
+        lanes = pl.ds(pl.multiple_of(lax.div(ep, 8) * LANES, LANES), LANES)
+        dm_full[...] = dot_tn(xg[:, lanes], dug[...])
+        dm_own[n] = dm_full[slice_rows, :]
+        mix_send(n)
 
     def mix_sum(n):
-        own = pl.ds(rows_at[SL][0][0], SL)
-        total = dm_full[n, slice_rows, :]
-        for r in range(1, 8):
+        total = dm_own[n]
+        for r in range(1, NDP):
             mix_copy(n, r).wait_recv()
             total = total + dm_recv[n, r - 1].astype(F32)
-        dm_all[n, own, :] = total.astype(BF)
-        for r in range(1, 8):
+        dm_all[n, own_slice, :] = total.astype(BF)
+        for r in range(1, NDP):
             mix_copy(n, r).wait_send()
 
+    def half_at(half):
+        return pl.ds(pl.multiple_of(half * (D // 2), D // 2), D // 2)
+
+    def slice_at(place):
+        return pl.ds(pl.multiple_of(place * SL, SL), SL)
+
+    def mix_gather_copy(n, r, place):
+        blk = dm_all.at[n, slice_at(place), half_at(core)]
+        return remote(blk, blk, mg_s.at[n, r], mg_r.at[n, r], ep_to=lax.rem(ep + r, NEP))
+
+    def mix_swap(n, half):
+        blk = dm_all.at[n, :, half_at(half)]
+        return remote(blk, blk, mg_s.at[n, 0], mg_r.at[n, 0], dp_to=partner)
+
+    def mix_gather_start(n):
+        @pl.loop(1, NEP)
+        def _(r):
+            mix_gather_copy(n, r, ep).start()
+
+    def mix_gather_done(n):
+        @pl.loop(1, NEP)
+        def _(r):
+            mix_gather_copy(n, r, lax.rem(ep + NEP - r, NEP)).wait_recv()
+            mix_gather_copy(n, r, ep).wait_send()
+
+        mix_swap(n, core).start()
+
+    def mix_swap_done(n):
+        mix_swap(n, 1 - core).wait_recv()
+        mix_swap(n, core).wait_send()
+
+    def mix_y_copy(j):
+        return remote(dm_part.at[:, unit_slice[j], :], dm_y.at[j - 1], ms_s.at[j], ms_r.at[j], ep_to=ep_of(0, j))
+
+    def mix_z_copy(i):
+        return remote(dm_mid.at[z_at[i]], dm_z.at[i - 1], ms_s.at[NY + i], ms_r.at[NY + i], ep_to=ep_of(i, 0))
+
+    def mix_scatter_start():
+        @pl.loop(0, NZ)
+        def _(i):
+            rows = pl.ds(pl.multiple_of(i * CH, CH), CH)
+            du1[rows, :] = pacc[rows, :].astype(BF)
+
+        du1[own_rows, :] = (pacc[own_rows, :] + dyg[z, home_unit, :].astype(F32)).astype(BF)
+
+        @pl.loop(0, 4)
+        def _(i):
+            rows = pl.ds(pl.multiple_of(i * LANES, LANES), LANES)
+            both_planes = dot_tn(x1[:, rows], du1[...]).astype(BF)
+            half = LANES // 2
+            dm_part[2 * i] = both_planes[:half]
+            dm_part[2 * i + 1] = both_planes[half:]
+
+        for j in range(1, NY):
+            mix_y_copy(j).start()
+
+    def mix_scatter_turn():
+        for j in range(1, NY):
+            mix_y_copy(j).wait_recv()
+
+        @pl.loop(0, NZ)
+        def _(i):
+            total = dm_part[i, unit_slice[0], :].astype(F32)
+            for j in range(1, NY):
+                total = total + dm_y[j - 1, i].astype(F32)
+            dm_mid[i] = total.astype(BF)
+
+        for i in range(1, NZ):
+            mix_z_copy(i).start()
+
+    def mix_scatter_sum():
+        total = dm_mid[z].astype(F32)
+        for i in range(1, NZ):
+            mix_z_copy(i).wait_recv()
+            total = total + dm_z[i - 1].astype(F32)
+        dm_own[0] = total
+        mix_send(0)
+
+    def mix_scatter_drain():
+        for j in range(1, NY):
+            mix_y_copy(j).wait_send()
+        for i in range(1, NZ):
+            mix_z_copy(i).wait_send()
+
+    unit_slice = [pl.ds(pl.multiple_of(yy * SL, SL), SL) for yy in y_at]
+    own_slice = slice_at(ep)
     own_rows = pl.ds(rows_at[T][0][0], T)
     home_unit = pl.ds(unit_at[0], T)
 
@@ -403,7 +498,7 @@
             table = table + jnp.where(slot == ids[j, l:l + 1, :] + 64 * l, gates[j, l:l + 1, :], 0.0)
     gt[own_rows, :] = table.T
     dyg[z, home_unit, :] = dout[...]
-    pl.semaphore_wait(barrier, len(peers))
+    pl.semaphore_wait(barrier, NEP + NDP - 2)
 
     def row_view(buf):
         return lambda dz, dy: buf.at[pl.ds(rows_at[T][dz][dy], T), :]
@@ -413,8 +508,6 @@
     ag_dy = ColumnGather()
     ag_x2 = Gather(row_view(x2), 0, 2)
     ag_du2 = Gather(row_view(du2), 1, 3)
-    ag_du1 = Gather(row_view(du1), 0, 4)
-    ag_mix = Gather(lambda dz, dy: dm_all.at[:, pl.ds(rows_at[SL][dz][dy], SL), :], 1, 5)
     ag_tok.start()
     ag_gt.start()
     ag_dy.start()
@@ -439,8 +532,8 @@
             def _(kk=kk):
                 ag_tok.chunk(kk)
                 ag_gt.chunk(kk)
-                if kk in (1, 3, 5, 7):
-                    ag_dy.zpoll((kk + 1) // 2)
+                if kk % 2:
+                    ag_dy.zpoll(kk // 2 + 1)
         rows = plane_rows(k)
         xc = x1[rows, :]
         u = (xc.astype(F32) + dot(xc, wmix[0])).astype(BF)
@@ -469,6 +562,7 @@
     y1 = (u1[own_rows, :].astype(F32) + rs.finish()).astype(BF)
     x2[own_rows, :] = y1
     ag_x2.start()
+    rs.drain()
 
     def backward_part(layer, e, rows, gcol, dyc, pre):
         a, b = pre[:, :FP], pre[:, FP:]
@@ -522,20 +616,20 @@
 
     rs = Scatter(pacc, 1)
     rs.round(0)
-    weight_grads(1, 0, u2)
-    rs.round(1)
-    weight_grads(1, 1, u2)
+    weight_grads(1, 1 - core, u2)
     ar2 = Reduce(1)
     ar2.stage(0)
-    for s in range(2, 5):
+    rs.round(1)
+    weight_grads(1, core, u2)
+    rs.round(2)
+    ar2.stage(1)
+    for s in range(3, 5):
         rs.round(s)
     rs.y_start()
     ag_x2.drain()
     du2[own_rows, :] = (dout[...].astype(F32) + rs.finish()).astype(BF)
     ag_du2.start()
-    ar2.stage(1)
-
-    rs_y2 = Scatter(pacc2, 3)
+    rs.drain()
 
     @pl.loop(0, 8)
     def _(k):
@@ -543,10 +637,12 @@
             @pl.when(k == kk)
             def _(kk=kk):
                 ag_du2.chunk(kk)
-                if kk in (2, 5):
-                    rs_y2.round(kk // 3)
+                if kk == 1:
+                    ar2.stage(2)
                 if kk == 4:
-                    ar2.stage(2)
+                    ar2.stage(3)
+                if kk == 7:
+                    ar2.stage(4)
         rows = plane_rows(k)
         duc = du2[rows, :]
         dyc = (duc.astype(F32) + dot_nt(duc, wmix[1])).astype(BF)
@@ -558,60 +654,54 @@
         pacc[rows, :] = back
 
     rs = Scatter(pacc, 2)
+    rs_y2 = Scatter(pacc2, 3)
     rs.round(0)
-    ar2.stage(3)
-    weight_grads(0, 0, u1)
-    rs.round(1)
-    weight_grads(0, 1, u1)
+    weight_grads(0, 1 - core, u1)
     ar1 = Reduce(0)
     ar1.stage(0)
-    rs_y2.round(2)
+    mix_scatter_start()
+    rs.round(1)
+    mix_start(1, x2, du2)
+    weight_grads(0, core, u1)
+    ar1.stage(1)
     rs.round(2)
-    mix_start(1, x2, du2)
-    ar1.stage(1)
+    mix_sum(1)
+    ar2.stage(5)
     rs.round(3)
-    ar2.stage(4)
-    rs_y2.round(3)
+    mix_scatter_turn()
     rs.round(4)
     rs.y_start()
-    ag_du2.drain()
-    mix_sum(1)
+    ar1.stage(2)
+    rs_y2.round(0)
+    ar2.stage(6)
     d_u1 = (dyg[z, home_unit, :].astype(F32) + rs.finish()).astype(BF)
-    du1[own_rows, :] = d_u1
-    ag_du1.start()
     dx_out[...] = (d_u1.astype(F32) + dot_nt(d_u1, wmix[0])).astype(BF)
-
+    mix_scatter_sum()
+    rs_y2.round(1)
+    mix_gather_start(1)
+    ar1.stage(3)
+    rs_y2.round(2)
+    mix_sum(0)
+    mix_gather_start(0)
+    rs_y2.round(3)
+    ar1.stage(4)
     rs_y2.round(4)
     rs_y2.y_start()
-    ag_du1.chunk(0)
-    ar2.stage(5)
-    for k in range(1, 4):
-        ag_du1.chunk(k)
-    ar1.stage(2)
-    for k in range(4, 6):
-        ag_du1.chunk(k)
-    ar2.stage(6)
-    for k in range(6, 8):
-        ag_du1.chunk(k)
-    mix_start(0, x1, du1)
+    ar2.stage(7)
+    ag_du2.drain()
+    rs.drain()
+    mix_scatter_drain()
+    mix_gather_done(1)
+    ar1.stage(5)
     y_out[...] = (u2[own_rows, :].astype(F32) + rs_y2.finish()).astype(BF)
-    ar1.stage(3)
-    mix_sum(0)
-    ag_mix.start()
-    for k in range(3):
-        ag_mix.chunk(k)
-    ar1.stage(4)
-    for k in range(3, 6):
-        ag_mix.chunk(k)
-    ar1.stage(5)
-    for k in range(6, 8):
-        ag_mix.chunk(k)
-    dmix_out[...] = dm_all[...]
+    mix_swap_done(1)
+    dmix_out[1] = dm_all[1]
+    mix_gather_done(0)
     ar1.stage(6)
-    ar2.stage(7)
+    mix_swap_done(0)
+    dmix_out[0] = dm_all[0]
+    rs_y2.drain()
     ar1.stage(7)
-    ag_du1.drain()
-    ag_mix.drain()
 
 
 def copy_kernel(*refs):
@@ -655,11 +745,14 @@
                 vmem((4, 2, CH, D)), vmem((4, 2, 3, CH, D)), vmem((4, 2, CH, D)),
                 vmem((4, 3, T, D)), vmem((4, 3, T, D)),
                 vmem(both(GR + 32, D)), vmem((2, GR, D)), vmem((2, 6, HR, LANES)), vmem(both(GR, D)),
-                vmem((2, LANES, D), F32), vmem((2, SL, D)), vmem((2, 7, SL, D)), vmem((2, D, D)),
+                vmem((LANES, D), F32), vmem((2, SL, D), F32), vmem((2, SL, D)), vmem((2, 7, SL, D)),
+                vmem((2, D, D)), vmem((NZ, NY * SL, D)), vmem((NZ, SL, D)),
+                vmem((NY, NZ, SL, D)), vmem((NZ, SL, D)),
                 dma((3, 2, 2)),
-                dma((2, 3)), dma((6, 3)), dma((2, *ZSEM)), dma((6, *ZSEM)),
+                dma((2, 3)), dma((4, 3)), dma((2, *ZSEM)), dma((4, *ZSEM)),
                 dma((2, *ZSEM)), dma((4, *ZSEM)), dma((2, 3)), dma((4, 3)),
-                dma((2, 12)), dma((2, 12)), dma((2, 7)), dma((2, 7)), dma((2, 2, 3)), dma((2, 6)), dma((2, 6)),
+                *[dma((2, 12))] * 2, *[dma((2, 7))] * 2, dma((2, 2, 3)), *[dma((2, 6))] * 2,
+                *[dma((2, NEP))] * 2, *[dma((NEP,))] * 2,
             ],
             compiler_params=pltpu.CompilerParams(
                 collective_id=0, has_side_effects=True, vmem_limit_bytes=67043328),

time: 196 us -> 179 us (0.913)
  Pallas kernels: 195 us -> 179 us
    pallas_call x1, Pallas kernels: 190 us -> 174 us  [device_step(): pl.pallas_call(step_kernel, out_shape=(shape((T, D), BF), shape((T, D), B...]
where the time goes in v2:
time: 179 us
  Pallas kernels  179 us (100%)
    pallas_call x1, Pallas kernels, device_step(): pl.pallas_call(step_kernel, out_shape=(shape((T, D), BF), shape((T, D), B...  174 us
    pallas_call x1, Pallas kernels, device_step(): pl.pallas_call(copy_kernel, out_shape=[shape(r.shape, r.dtype) for r in r...  4.76 us

profile of v2, /device:TPU:1, one launch (start us, length us, event | category | flops | bytes accessed | tf_op | source)
XLA Modules:
  0.0 179.4 jit_solution(12725004323231362056)
XLA Ops:
  0.6 174.0 %shard_map.127 = (bf16[32,512]{1,0:T(8,128)(2,1)}, bf16[32,512]{1,0:T(8,128)(2,1)}, bf16[2,512,512]{2,1,0:T(8,128)(2,1)}, bf16[2,2,352,512]{3,2,1,0:T(8,128)(2,1...) custom-call(bf16[32,512]{1,0:T(8,128)(2,1)} %tok.1, bf16[32,512]{1,0:T(8,128)(2,1)} %dout.1, ...), custom_call_target="tpu_custom_call" | custom-call | tf_op jit(solution)/shard_map/pallas_call | solution.py:733
  174.6 4.8 %shard_map.128 = (bf16[32,512]{1,0:T(8,128)(2,1)}, bf16[32,512]{1,0:T(8,128)(2,1)}, bf16[2,512,512]{2,1,0:T(8,128)(2,1)}, bf16[2,2,352,512]{3,2,1,0:T(8,128)(2,1...) custom-call(bf16[32,512]{1,0:T(8,128)(2,1)} %get-tuple-element.18.refs_0_, ...), custom_call_target="tpu_custom_call" | custom-call | tf_op jit(solution)/shard_map/pallas_call | solution.py:761

commit v3 on v2

--- a/solution.py
+++ b/solution.py
@@ -90,13 +90,10 @@
             device_id_type=MESH)
 
     barrier = pltpu.get_barrier_semaphore()
-
-    @pl.loop(1, NEP)
-    def _(r):
-        pl.semaphore_signal(barrier, inc=1, device_id=(lax.rem(ep + r, NEP), dp), device_id_type=MESH)
-
-    for r in range(1, NDP):
-        pl.semaphore_signal(barrier, inc=1, device_id=(ep, dp_r[r]), device_id_type=MESH)
+    peers = [(ep_of(0, j), dp) for j in range(1, NY)] + [(ep_of(sign, 0), dp) for sign in SIGN]
+    peers += [(ep, place) for place in dp_r[1:]]
+    for peer in peers:
+        pl.semaphore_signal(barrier, inc=1, device_id=peer, device_id_type=MESH)
 
     loads = []
     for p, src in enumerate((wg_hbm, wu_hbm, wd_hbm)):
@@ -498,7 +495,7 @@
             table = table + jnp.where(slot == ids[j, l:l + 1, :] + 64 * l, gates[j, l:l + 1, :], 0.0)
     gt[own_rows, :] = table.T
     dyg[z, home_unit, :] = dout[...]
-    pl.semaphore_wait(barrier, NEP + NDP - 2)
+    pl.semaphore_wait(barrier, len(peers))
 
     def row_view(buf):
         return lambda dz, dy: buf.at[pl.ds(rows_at[T][dz][dy], T), :]
@@ -553,16 +550,17 @@
     rs = Scatter(pacc, 0)
     for s in range(5):
         rs.round(s)
-        if s in (2, 4):
-            ag_dy.ypoll(s // 2)
+        if s == 1:
+            ag_dy.ypoll(1)
     rs.y_start()
     ag_tok.drain()
     ag_gt.drain()
-    ag_dy.drain()
     y1 = (u1[own_rows, :].astype(F32) + rs.finish()).astype(BF)
     x2[own_rows, :] = y1
     ag_x2.start()
     rs.drain()
+    ag_dy.ypoll(2)
+    ag_dy.drain()
 
     def backward_part(layer, e, rows, gcol, dyc, pre):
         a, b = pre[:, :FP], pre[:, FP:]

time: 179 us -> 177 us (0.989)
  Pallas kernels: 179 us -> 177 us
    pallas_call x1, Pallas kernels: 174 us -> 172 us  [device_step(): pl.pallas_call(step_kernel, out_shape=(shape((T, D), BF), shape((T, D), B...]
where the time goes in v3:
time: 177 us
  Pallas kernels  177 us (100%)
    pallas_call x1, Pallas kernels, device_step(): pl.pallas_call(step_kernel, out_shape=(shape((T, D), BF), shape((T, D), B...  172 us
    pallas_call x1, Pallas kernels, device_step(): pl.pallas_call(copy_kernel, out_shape=[shape(r.shape, r.dtype) for r in r...  4.76 us

profile of v3, /device:TPU:1, one launch (start us, length us, event | category | flops | bytes accessed | tf_op | source)
XLA Modules:
  0.0 177.4 jit_solution(11833668086152384255)
XLA Ops:
  0.6 172.0 %shard_map.127 = (bf16[32,512]{1,0:T(8,128)(2,1)}, bf16[32,512]{1,0:T(8,128)(2,1)}, bf16[2,512,512]{2,1,0:T(8,128)(2,1)}, bf16[2,2,352,512]{3,2,1,0:T(8,128)(2,1...) custom-call(bf16[32,512]{1,0:T(8,128)(2,1)} %tok.1, bf16[32,512]{1,0:T(8,128)(2,1)} %dout.1, ...), custom_call_target="tpu_custom_call" | custom-call | tf_op jit(solution)/shard_map/pallas_call | solution.py:731
  172.6 4.8 %shard_map.128 = (bf16[32,512]{1,0:T(8,128)(2,1)}, bf16[32,512]{1,0:T(8,128)(2,1)}, bf16[2,512,512]{2,1,0:T(8,128)(2,1)}, bf16[2,2,352,512]{3,2,1,0:T(8,128)(2,1...) custom-call(bf16[32,512]{1,0:T(8,128)(2,1)} %get-tuple-element.18.refs_0_, ...), custom_call_target="tpu_custom_call" | custom-call | tf_op jit(solution)/shard_map/pallas_call | solution.py:759
